TPU v7x, 256 devices: a whole 4x4x8 slice. The times are simulated.
256 devices in a mesh: row: 16 (over x_hi, y, core), col: 16 (over x_lo, z).
Axes of the slice: x: 4 (x_hi: 2, x_lo: 2; x = x_hi * 2 + x_lo), y: 4, z: 8, core: 2. Of those that a mesh axis runs over, the one named last changes fastest.
Arguments:
- gradient: float32 [4096, 4608], P('row', 'col'), may hold values from -12 to 12
- first_moment: float32 [4096, 4608], P('row', 'col'), may hold values from -12 to 12, as said below
- second_moment: float32 [4096, 4608], P('row', 'col'), may hold values from 0.01 to 1
- weights: float32 [4096, 4608], P('row', 'col'), may hold values from -6 to 6
- eigenbasis: float32 [4608, 4608], P('row', 'col'), may hold values from -1 to 1, as said below
Outputs:
- new_weights: float32 [4096, 4608], P('row', 'col')
- new_first: float32 [4096, 4608], P('row', 'col')
- new_second: float32 [4096, 4608], P('row', 'col')
Inputs may be any that keep to these rules, and one draw needn't show every extreme that they name: `first_moment`: every entry's magnitude is at most 12. eigenbasis is orthogonal: its columns are orthonormal.
All inputs are finite; a program needn't handle non-finite values.
Results may differ from a plain program's by a relative error of at most 0.000059.
Values sent between devices are 32-bit elements; how exact they have to be, the bound alone decides.
A program may use at most 64 MiB of HBM per device.

v0:
```python
import jax.numpy as jnp
from jax import lax

D = 4608


bias_first = 1.0 - 0.9**10


bias_second = 1.0 - 0.999**10


epsilon = 1e-08


step_rate = 0.25


def reference(gradient, first_moment, second_moment, weights, eigenbasis):
    highest = lax.Precision.HIGHEST
    rotated = jnp.dot(gradient, eigenbasis, precision=highest, preferred_element_type=jnp.float32)
    new_first = 0.9 * first_moment + 0.1 * rotated
    new_second = 0.999 * second_moment + 0.001 * rotated * rotated
    direction = new_first / bias_first / (jnp.sqrt(new_second / bias_second) + epsilon)
    row_rms = jnp.sqrt(jnp.sum(direction * direction, axis=1, keepdims=True) / D)
    update = jnp.dot(direction, eigenbasis.T, precision=highest, preferred_element_type=jnp.float32)
    new_weights = weights - step_rate * update / jnp.maximum(1.0, row_rms)
    return (new_weights, new_first, new_second)


def solution(mesh):
    return reference
```

profile of v0, /device:TPU:8, one launch (start us, length us, event | category | flops | bytes accessed | tf_op | source)
XLA Modules:
  0.0 276.4 jit_solution(12285366308595003030)
XLA Ops:
  7.2 0.0 all-gather.7.cloned.1.call-start
  7.2 0.7 all-gather.7.cloned.1.call-update
  7.9 0.0 all-gather.9.cloned.1.call-start
  7.9 0.7 all-gather.9.cloned.1.call-update
  8.6 0.0 reduce-scatter.4.cloned.1.call-start
  8.7 80.7 %all-gather.7.cloned.1.call-done = f32[256,4608]{0,1:T(8,128)} async-done(((f32[256,288]{0,1:T(8,128)}), f32[256,4608]{0,1:T(8,128)}) %all-gather.7.cloned.1.call-update) | async-done | bytes 4718608 | tf_op args[0]
  89.4 70.7 %all-gather.9.cloned.1.call-done = f32[4608,288]{1,0:T(8,128)} async-done(((f32[288,288]{1,0:T(8,128)}), f32[4608,288]{1,0:T(8,128)}) %all-gather.9.cloned.1.call-update) | async-done | bytes 5308432 | tf_op args[4]
  160.1 0.0 copy-start
  160.1 16.0 %multiply_reduce_fusion = (f32[256]{0:T(256)S(1)}, f32[256,288]{0,1:T(8,128)S(1)}, f32[256,288]{0,1:T(8,128)S(1)}) fusion(f32[256,288]{0,1:T(8,128)} %param.1, f32[256,288]{0,1:T(8,128)} %param.4, f32[256,4608]{0,1:T(8,128)} %all-gather.7.cloned.1.call-done, f32[4608,288]{1,0:T(8,128)} %all-gather.9.cloned.1.call-done), kind=kOutput, calls=%fused_computation.3 | convolution fusion | flops 4077821696 | bytes 11207680 | tf_op jit(solution)/dot_general | solution.py:21
  176.1 0.0 copy-start.1
  176.2 0.0 copy-start.2
  176.2 0.0 copy-done
  176.2 0.0 copy-start.3
  176.2 9.9 %fusion.1 = f32[256,4608]{0,1:T(8,128)} fusion(f32[4608,288]{1,0:T(8,128)S(1)} %copy-done, f32[256,288]{0,1:T(8,128)S(1)} %get-tuple-element.2, f32[256,288]{0,1:T(8,128)S(1)} %get-tuple-element.1), kind=kOutput, calls=%fused_computation.7 | convolution fusion | flops 4077158400 | bytes 10616832 | tf_op jit(solution)/dot_general | solution.py:26
  186.1 0.0 copy-done.1
  186.1 0.0 copy-done.2
  186.1 0.0 reduce-scatter.4.cloned.1.call-update
  186.1 34.3 %all-reduce.1 = f32[256]{0:T(256)S(1)} all-reduce(f32[256]{0:T(256)S(1)} %get-tuple-element), channel_id=6, replica_groups=mesh['axis_0'=16,'axis_1'=16] {'axis_1'}, use_global_device_ids=true, to_apply=%region_0.0.clone | all-reduce | flops 256 | bytes 2048 | tf_op jit(solution)/reduce_sum | solution.py:25
  220.4 47.7 %reduce-scatter.4.cloned.1.call-done = f32[256,288]{0,1:T(8,128)} async-done(((f32[256,4608]{0,1:T(8,128)}), f32[256,288]{0,1:T(8,128)}) %reduce-scatter.4.cloned.1.call-update) | async-done | bytes 294928
  268.1 0.0 copy-done.3
  268.1 1.7 divide_subtract_fusion
  (1 shorter events, 0.0 us)
Async XLA Ops:
  7.2 82.3 %all-gather.7.cloned.1.call-start = ((), (), s32[]{:S(2)}) async-start(), calls=%async_computation.1 | async-start | bytes 5013504 | tf_op args[0]
  7.9 152.2 %all-gather.9.cloned.1.call-start = ((), (), s32[]{:S(2)}) async-start(), calls=%async_computation.2 | async-start | bytes 7520256 | tf_op args[4]
  8.6 259.5 %reduce-scatter.4.cloned.1.call-start = ((), (), s32[]{:S(2)}) async-start(), calls=%async_computation.3 | async-start | bytes 5013504
  160.1 16.1 %copy-start = (f32[4608,288]{1,0:T(8,128)S(1)}, f32[4608,288]{1,0:T(8,128)}, u32[]{:S(2)}) copy-start(f32[4608,288]{1,0:T(8,128)} %all-gather.9.cloned.1.call-done) | copy-start | bytes 15925252
  176.1 9.9 %copy-start.1 = (f32[256,288]{0,1:T(8,128)}, f32[256,288]{0,1:T(8,128)S(1)}, u32[]{:S(2)}) copy-start(f32[256,288]{0,1:T(8,128)S(1)} %get-tuple-element.1) | copy-start | bytes 884740
  176.2 9.9 %copy-start.2 = (f32[256,288]{0,1:T(8,128)}, f32[256,288]{0,1:T(8,128)S(1)}, u32[]{:S(2)}) copy-start(f32[256,288]{0,1:T(8,128)S(1)} %get-tuple-element.2) | copy-start | bytes 884740
  176.2 91.9 %copy-start.3 = (f32[256,288]{0,1:T(8,128)S(1)}, f32[256,288]{0,1:T(8,128)}, u32[]{:S(2)}) copy-start(f32[256,288]{0,1:T(8,128)} %param) | copy-start | bytes 884740
Sparse Core Ops, SparseCore 0:
  9.8 79.6 all-gather.6
  92.2 67.8 all-gather.8
  186.2 81.8 reduce-scatter.3
where the time goes:
time: 277 us; the launch traced here: 276 us
  waiting for transfers between devices  201 us (73%)
  blocking collectives  34.3 us (12%)
  matrix products  25.9 us (9%)
  between operations  13.8 us (5%)
    unnamed x6, waiting for transfers between devices  201 us
    reduce_sum x1, blocking collectives, reference(): jnp.sum(direction * direction, axis=1, keepdims=True) / D  34.3 us
    dot_general x1, matrix products, reference(): jnp.dot(gradient, eigenbasis, precision=highest, preferred_element_type=j...  16 us
    dot_general x1, matrix products, reference(): jnp.dot(direction, eigenbasis.T, precision=highest, preferred_element_typ...  9.86 us
  transfers between devices with their start and end apart: 3, of which 3 were waited for; matrix products, arithmetic and copies ran while one was open for 0% of the time, Pallas kernels for 0%

commit v1 on v0

v1 whole, which is shorter than its diff:
```python
import jax
import jax.numpy as jnp
from jax import lax
from jax.experimental import pallas as pl
from jax.experimental.pallas import tpu as pltpu
from jax.sharding import PartitionSpec as P

MESH = pl.DeviceIdType.MESH
D = 4608
bias_first = 1.0 - 0.9**10
bias_second = 1.0 - 0.999**10
epsilon = 1e-08
step_rate = 0.25

B = 288
M = 256
NB = 16
Q_HALF = ((0, 328), (328, 320))
G_HALF = ((0, 144), (144, 144))
U_HALF = ((0, 152), (152, 144))
NSEND = 128


def split(v):
    hi = v.astype(jnp.bfloat16)
    return hi, (v - hi.astype(jnp.float32)).astype(jnp.bfloat16)


def dot3(ah, al, bh, bl, dims):
    def one(p, q):
        return lax.dot_general(p, q, (dims, ((), ())), preferred_element_type=jnp.float32)

    return one(ah, bh) + (one(ah, bl) + one(al, bh))


def kernel(g, q, m1, m2, rot_o, upd_o, gbuf, qbuf, qstage, qh, ql, mbuf, acc, ustage, dh, dl, osend, ubuf, dbuf, rbuf, ss, qs, gs, ms, ds, rs, us):
    row, col = lax.axis_index("row"), lax.axis_index("col")
    xh, y, b = row // 8, lax.rem(row // 2, 4), lax.rem(row, 2)
    a, z = col // 8, lax.rem(col, 8)
    x = 2 * xh + a
    o = 1 - b
    cond = {"S": a == b, "N": a != b}
    xp, xm = lax.rem(x + 1, 4), lax.rem(x + 3, 4)
    yy = {d: lax.rem(y + d + 4, 4) for d in (0, 1, -1, 2)}
    zz = {d: lax.rem(z + d + 8, 8) for d in range(-4, 5)}

    def dev(x_, y_, z_, c_):
        return ((x_ // 2) * 8 + y_ * 2 + c_, lax.rem(x_, 2) * 8 + z_)

    to = {
        "x+": dev(xp, y, z, b),
        "x-": dev(xm, y, z, b),
        "y+": dev(x, yy[1], z, b),
        "y-": dev(x, yy[-1], z, b),
        "z+": dev(x, y, zz[1], b),
        "z-": dev(x, y, zz[-1], b),
        "core": dev(x, y, z, o),
        "swap": dev(2 * xh + b, y, z, o),
    }

    def on(tag, f):
        if tag is None:
            f()
        else:
            pl.when(cond[tag])(f)

    sends = []

    def send(tag, src, dst, rsem, where):
        k = len(sends)

        def make():
            return pltpu.make_async_remote_copy(
                src_ref=src(), dst_ref=dst(), send_sem=ss.at[k], recv_sem=rsem(), device_id=to[where], device_id_type=MESH
            )

        make().start()
        sends.append((tag, make))

    def arrived(ref, sem):
        pltpu.make_async_copy(ref, ref, sem).wait()

    def blk(h, d, c):
        return h * 8 + yy[d] * 2 + c

    def q_part(i, half):
        return qbuf.at[i, pl.ds(*Q_HALF[half]), :]

    def q_send(tag, i, half, *wheres):
        for w in wheres:
            send(tag, lambda: q_part(i(), half), lambda: q_part(i(), half), lambda: qs.at[i(), half], w)

    def q_wait(i, half):
        arrived(q_part(i(), half), qs.at[i(), half])

    def g_part(c, d, half):
        return gbuf.at[c * 8 + zz[d], pl.ds(*G_HALF[half]), :]

    def g_send(tag, d, half, *wheres, src=None):
        for w in wheres:
            s = (lambda: g.at[pl.ds(*G_HALF[half]), :]) if src else (lambda: g_part(b, d, half))
            send(tag, s, lambda: g_part(b, d, half), lambda: gs.at[b * 8 + zz[d], half], w)

    def g_wait(c, d, half):
        arrived(g_part(c, d, half), gs.at[c * 8 + zz[d], half])

    def pack(put):
        put(0, B, q[:, 0:128])
        put(B, B, q[:, 128:256])
        put(2 * B, 72, jnp.concatenate([q[72 * i : 72 * i + 72, 256:288] for i in range(4)], axis=1))

    def pack_own():
        def put(at, n, v):
            qbuf[row, at : at + n, :] = v

        pack(put)

    def pack_stage():
        def put(at, n, v):
            qstage[at : at + n, :] = v

        pack(put)

    barrier = pltpu.get_barrier_semaphore()
    for w in ("x+", "x-", "y+", "y-", "z+", "z-", "core"):
        pl.semaphore_signal(barrier, inc=1, device_id=to[w], device_id_type=MESH)

    @pl.when(cond["N"])
    def _():
        pl.semaphore_signal(barrier, inc=1, device_id=to["swap"], device_id_type=MESH)

    on("S", pack_own)
    on("N", pack_stage)
    on("S", lambda: pl.semaphore_wait(barrier, 7))
    on("N", lambda: pl.semaphore_wait(barrier, 8))

    own = lambda: row
    mate = lambda: blk(xh, 0, o)
    far = lambda d, c: (lambda: blk(1 - xh, d, c))
    left = lambda d, c: (lambda: blk(xm // 2, d, c))
    right = lambda d, c: (lambda: blk(xp // 2, d, c))
    mine = lambda d, c: (lambda: blk(xh, d, c))

    def local(k, half):
        return pltpu.make_async_copy(g.at[pl.ds(*G_HALF[half]), :], g_part(b, 0, half), gs.at[b * 8 + z, half])

    def e0_s():
        for half in (0, 1):
            local(0, half).start()
        q_send("S", own, 0, "x+", "x-")
        q_send("S", own, 1, "y+", "y-")
        for half in (0, 1):
            g_send("S", 0, half, "z+", "z-", "core", src=True)
        pltpu.make_async_copy(m1, mbuf.at[0], ms.at[0]).start()
        pltpu.make_async_copy(m2, mbuf.at[1], ms.at[1]).start()

    def e0_n():
        def hand_q(half):
            send("N", lambda: qstage.at[pl.ds(*Q_HALF[half]), :], lambda: q_part(row, half), lambda: qs.at[row, half], "core")

        def hand_g(half):
            send("N", lambda: g.at[pl.ds(*G_HALF[half]), :], lambda: g_part(o, 0, half), lambda: gs.at[o * 8 + z, half], "swap")

        hand_q(0)
        hand_q(1)
        hand_g(0)
        hand_g(1)

    on("S", e0_s)
    on("N", e0_n)

    def e1_s():
        q_wait(mate, 0)
        q_send("S", mate, 0, "x+", "x-")
        q_wait(mate, 1)
        q_send("S", mate, 1, "y+", "y-")
        for i in (own, mate):
            q_send("S", i, 1, "x+", "x-")
            q_send("S", i, 0, "y+", "y-")

    def z0_n():
        for half in (0, 1):
            g_wait(b, 0, half)
            g_send("N", 0, half, "z+", "z-", "core")

    def e2_n():
        q_wait(left(0, 0), 0)
        q_send("N", left(0, 0), 0, "x+", "y+", "y-")
        q_wait(right(0, 1), 0)
        q_send("N", right(0, 1), 0, "x-", "y+", "y-")
        q_wait(left(0, 1), 0)
        q_send("N", left(0, 1), 0, "y+", "y-")
        q_wait(right(0, 0), 0)
        q_send("N", right(0, 0), 0, "y+", "y-")
        send("N", lambda: m1, lambda: mbuf.at[0], lambda: ms.at[0], "swap")
        send("N", lambda: m2, lambda: mbuf.at[1], lambda: ms.at[1], "swap")

    def e3_s():
        q_wait(mine(-1, 0), 1)
        q_send("S", mine(-1, 0), 1, "y+", "x+", "x-")
        q_wait(mine(1, 1), 1)
        q_send("S", mine(1, 1), 1, "y-", "x+", "x-")
        q_wait(mine(-1, 1), 1)
        q_send("S", mine(-1, 1), 1, "x+", "x-")
        q_wait(mine(1, 0), 1)
        q_send("S", mine(1, 0), 1, "x+", "x-")

    def z_event(d):
        for way, back, first in (("+", -d, 0), ("-", d, 1)):
            for half in (first, 1 - first):
                hops = 4 if half == first else 3
                if d > hops:
                    continue
                g_wait(b, back, half)
                g_send(None, back, half, *((["z" + way] if d < hops else []) + ["core"]))

    def e4_s():
        for c in (0, 1):
            q_wait(far(0, c), 0)
            q_send("S", far(0, c), 0, "y+", "y-")

    def n_b(d, side=None):
        for i, way, c in ((left, "x+", 0), (right, "x-", 1), (left, None, 1), (right, None, 0)):
            q_wait(i(d, c), 1)
            if way:
                q_send("N", i(d, c), 1, way)

    def a_ring():
        for h in (lambda: xh, lambda: 1 - xh):
            for d, way, c in ((-1, "y+", 0), (1, "y-", 1), (-1, None, 1), (1, None, 0)):
                i = lambda h=h, d=d, c=c: blk(h(), d, c)
                q_wait(i, 0)
                if way:
                    q_send(None, i, 0, way)

    def e6_s():
        for c in (0, 1):
            q_wait(mine(2, c), 1)
            q_send("S", mine(2, c), 1, "x+", "x-")

    def s_far(d):
        for c in (0, 1):
            q_wait(far(d, c), 1)

    on("S", e1_s)
    on("N", z0_n)
    on("N", e2_n)
    on("S", e3_s)
    z_event(1)
    on("S", e4_s)
    on("N", lambda: n_b(0))
    z_event(2)
    a_ring()
    on("S", e6_s)
    on("S", lambda: s_far(0))
    z_event(3)

    def n_b1():
        n_b(-1)
        n_b(1)

    on("N", n_b1)
    z_event(4)

    @pl.when(cond["S"])
    def _():
        for half in (0, 1):
            g_wait(b, 0, half)
        s_far(1)
        s_far(-1)

    for d in (0, 1, -1, 2, -2, 3, -3, 4):
        for half in (0, 1):
            g_wait(o, d, half)

    acc[...] = jnp.zeros_like(acc)

    def group(d):
        def body(i, c):
            k = (i // 2) * 8 + yy[d] * 2 + lax.rem(i, 2)
            tail = qbuf[k, 2 * B : 2 * B + 72, :]
            tail = jnp.concatenate([tail[:, 32 * j : 32 * j + 32] for j in range(4)], axis=0)
            block = jnp.concatenate([qbuf[k, 0:B, :], qbuf[k, B : 2 * B, :], tail], axis=1)
            hi, lo = split(block)
            qh[k] = hi
            ql[k] = lo
            gh, gl = split(gbuf[k])
            acc[...] += dot3(hi, lo, gh, gl, ((0,), (0,)))
            return c

        lax.fori_loop(0, 4, body, 0)

    group(0)
    group(1)
    group(-1)

    on("N", lambda: n_b(2))
    for h in (0, 1):
        for c in (0, 1):
            q_wait(lambda: blk(h, 2, c), 0)
    on("S", lambda: s_far(2))
    group(2)

    on("S", lambda: rot_o.__setitem__(..., acc[...]))

    @pl.when(cond["N"])
    def _():
        send("N", lambda: acc, lambda: rot_o, lambda: us.at[2], "swap")

    arrived(mbuf.at[0], ms.at[0])
    arrived(mbuf.at[1], ms.at[1])
    rot = acc[...]
    new_first = 0.9 * mbuf[0] + 0.1 * rot
    new_second = 0.999 * mbuf[1] + 0.001 * rot * rot
    direction = new_first / bias_first / (jnp.sqrt(new_second / bias_second) + epsilon)
    hi, lo = split(direction)
    dh[...] = hi
    dl[...] = lo
    sums = jnp.broadcast_to(jnp.sum(direction * direction, axis=0, keepdims=True), (8, M))

    def product(c, d, buf):
        j = c * 8 + zz[d]
        buf[d % 8, 0:8, :] = sums
        buf[d % 8, 8:, :] = dot3(qh[j], ql[j], dh[...], dl[...], ((1,), (0,)))

    def other(d):
        product(o, d, osend)
        send(None, lambda: osend.at[d % 8], lambda: dbuf.at[d % 8], lambda: ds.at[d % 8], "core")

    def self_(d):
        product(b, d, ubuf)

    def chain(d):
        i = d % 8
        arrived(dbuf.at[i], ds.at[i])
        ways = {4: (("+", 0), ("-", 1)), 3: (("+", 0), ("+", 1)), 2: (("+", 0), ("+", 1)), 1: (("+", 0), ("+", 1))}
        todo = ways[d] if d > 0 else (("-", 1), ("-", 0))
        far_ = abs(d)

        def link(way, half):
            at, n = U_HALF[half]
            s = 0 if way == "+" else 1
            start = 4 if half == s else 3
            v = ubuf[i, at : at + n, :] + dbuf[i, at : at + n, :]
            if far_ < start:
                k = start - 1 - far_
                arrived(rbuf.at[s, half, k, pl.ds(0, n), :], rs.at[s, half, k])
                v = v + rbuf[s, half, k, 0:n, :]
            ubuf[i, at : at + n, :] = v
            k = start - far_
            send(
                None,
                lambda: ubuf.at[i, pl.ds(at, n), :],
                lambda: rbuf.at[s, half, k, pl.ds(0, n), :],
                lambda: rs.at[s, half, k],
                "z" + way,
            )

        for way, half in todo:
            link(way, half)

    other(4)
    self_(4)
    other(3)
    other(-3)
    chain(4)
    self_(3)
    self_(-3)
    chain(3)
    chain(-3)
    other(2)
    other(-2)
    self_(2)
    self_(-2)
    chain(2)
    chain(-2)
    other(1)
    other(-1)
    self_(1)
    self_(-1)
    other(0)
    self_(0)
    chain(1)
    chain(-1)

    arrived(dbuf.at[0], ds.at[0])

    def total(half):
        at, n = U_HALF[half]
        v = ubuf[0, at : at + n, :] + dbuf[0, at : at + n, :]
        for s in (0, 1):
            k = (4 if half == s else 3) - 1
            arrived(rbuf.at[s, half, k, pl.ds(0, n), :], rs.at[s, half, k])
            v = v + rbuf[s, half, k, 0:n, :]
        return v

    first = total(0)
    limit = jnp.maximum(1.0, jnp.sqrt(first[0:1] / D))

    def finish(half, v):
        def keep():
            upd_o[pl.ds(*G_HALF[half]), :] = v

        def hand():
            ustage[pl.ds(*G_HALF[half]), :] = v
            send(
                "N",
                lambda: ustage.at[pl.ds(*G_HALF[half]), :],
                lambda: upd_o.at[pl.ds(*G_HALF[half]), :],
                lambda: us.at[half],
                "swap",
            )

        on("S", keep)
        on("N", hand)

    finish(0, step_rate * first[8:] / limit)
    finish(1, step_rate * total(1) / limit)

    @pl.when(cond["N"])
    def _():
        arrived(rot_o, us.at[2])
        for half in (0, 1):
            arrived(upd_o.at[pl.ds(*G_HALF[half]), :], us.at[half])

    for tag in ("S", "N"):

        @pl.when(cond[tag])
        def _():
            for t, make in sends:
                if t == tag:
                    make().wait_send()

    for t, make in sends:
        if t is None:
            make().wait_send()


def solution(mesh):
    def step(gradient, first_moment, second_moment, weights, eigenbasis):
        m1, m2, w = first_moment.T, second_moment.T, weights.T
        f32, bf16 = jnp.float32, jnp.bfloat16
        vmem = pl.BlockSpec(memory_space=pltpu.VMEM)
        hbm = pl.BlockSpec(memory_space=pl.ANY)
        dma = pltpu.SemaphoreType.DMA
        rot, upd = pl.pallas_call(
            kernel,
            out_shape=[jax.ShapeDtypeStruct((B, M), f32)] * 2,
            in_specs=[vmem, vmem, hbm, hbm],
            out_specs=[vmem, vmem],
            scratch_shapes=[
                pltpu.VMEM((NB, B, M), f32),
                pltpu.VMEM((NB, 648, 128), f32),
                pltpu.VMEM((648, 128), f32),
                pltpu.VMEM((NB, B, B), bf16),
                pltpu.VMEM((NB, B, B), bf16),
                pltpu.VMEM((2, B, M), f32),
                pltpu.VMEM((B, M), f32),
                pltpu.VMEM((B, M), f32),
                pltpu.VMEM((B, M), bf16),
                pltpu.VMEM((B, M), bf16),
                pltpu.VMEM((8, B + 8, M), f32),
                pltpu.VMEM((8, B + 8, M), f32),
                pltpu.VMEM((8, B + 8, M), f32),
                pltpu.VMEM((2, 2, 4, 152, M), f32),
                dma((NSEND,)),
                dma((NB, 2)),
                dma((NB, 2)),
                dma((2,)),
                dma((8,)),
                dma((2, 2, 4)),
                dma((3,)),
            ],
            compiler_params=pltpu.CompilerParams(collective_id=0, has_side_effects=True, vmem_limit_bytes=56 * 2**20),
        )(gradient.T, eigenbasis, m1, m2)
        new_first = 0.9 * m1 + 0.1 * rot
        new_second = 0.999 * m2 + 0.001 * rot * rot
        new_weights = w - upd
        return new_weights.T, new_first.T, new_second.T

    spec = P("row", "col")
    return jax.shard_map(step, mesh=mesh, in_specs=(spec,) * 5, out_specs=(spec,) * 3, check_vma=False)
```

time: 277 us -> 97 us (0.35)
  the two profiles are of different devices: /device:TPU:8 before, /device:TPU:1 now
where the time goes in v1:
time: 97 us; the launch traced here: 96.9 us
  Pallas kernels  94.2 us (97%)
  other arithmetic  2.01 us (2%)
    pallas_call x1, Pallas kernels, step(): pl.pallas_call(kernel, out_shape=[jax.ShapeDtypeStruct((B, M), f32)] * 2,...  94.2 us
    transpose x1, other arithmetic, step(): return (new_weights.T, new_first.T, new_second.T)  2.01 us

profile of v1, /device:TPU:1, one launch (start us, length us, event | category | flops | bytes accessed | tf_op | source)
XLA Modules:
  0.0 96.9 jit_solution(15537474623000283323)
XLA Ops:
  0.6 0.0 copy-start
  0.6 0.0 copy-start.1
  0.7 0.0 copy-start.2
  0.7 94.2 %shard_map.76 = (f32[288,256]{1,0:T(8,128)}, f32[288,256]{1,0:T(8,128)}) custom-call(f32[288,256]{1,0:T(8,128)} %bitcast.17, f32[288,288]{1,0:T(8,128)} %q.1, f32[288,256]{1,0:T(8,128)} %bitcast.15, f32[288,256]{1,0:T(8,128)} %bitcast.16), custom_call_target="tpu_custom_call" | custom-call | tf_op jit(solution)/shard_map/pallas_call | solution.py:446
  94.9 0.0 copy-done
  94.9 0.0 copy-done.1
  94.9 0.0 copy-done.2
  94.9 2.0 %fusion.1 = (f32[256,288]{0,1:T(8,128)}, f32[256,288]{0,1:T(8,128)}, f32[256,288]{0,1:T(8,128)}) fusion(f32[288,256]{1,0:T(8,128)} %get-tuple-element.6, f32[256,288]{0,1:T(8,128)S(1)} %copy-done.1, f32[256,288]{0,1:T(8,128)S(1)} %copy-done, f32[288,256]{1,0:T(8,128)} %get-tuple-element.5, f32[256,288]{0,1:T(8,128)S(1)} %copy-done.2), kind=kLoop, calls=%fused_computation.2 | loop fusion | flops 589824 | bytes 2359296 | tf_op jit(solution)/shard_map/transpose | solution.py:479
Async XLA Ops:
  0.6 94.3 %copy-start = (f32[256,288]{0,1:T(8,128)S(1)}, f32[256,288]{0,1:T(8,128)}, u32[]{:S(2)}) copy-start(f32[256,288]{0,1:T(8,128)} %param.6) | copy-start | bytes 884740
  0.6 94.3 %copy-start.1 = (f32[256,288]{0,1:T(8,128)S(1)}, f32[256,288]{0,1:T(8,128)}, u32[]{:S(2)}) copy-start(f32[256,288]{0,1:T(8,128)} %param.7) | copy-start | bytes 884740
  0.7 94.3 %copy-start.2 = (f32[256,288]{0,1:T(8,128)S(1)}, f32[256,288]{0,1:T(8,128)}, u32[]{:S(2)}) copy-start(f32[256,288]{0,1:T(8,128)} %param.8) | copy-start | bytes 884740

commit v2 on v0

v2 whole, which is shorter than its diff:
```python
import jax
import jax.numpy as jnp
from jax import lax
from jax.experimental import pallas as pl
from jax.experimental.pallas import tpu as pltpu
from jax.sharding import PartitionSpec as P

MESH = pl.DeviceIdType.MESH
D = 4608
bias_first = 1.0 - 0.9**10
bias_second = 1.0 - 0.999**10
epsilon = 1e-08
step_rate = 0.25

B = 288
M = 256
NB = 16
Q_HALF = ((0, 376), (376, 272))
G_PART = ((0, 72), (72, 72), (144, 72), (216, 72))
U_PART = ((0, 80), (80, 72), (152, 72), (224, 72))
FAR_SIDE = ((0, 1), (2, 3))
NSEND = 288


def split(v):
    hi = v.astype(jnp.bfloat16)
    return hi, (v - hi.astype(jnp.float32)).astype(jnp.bfloat16)


def dot(p, q):
    return jnp.dot(p, q, preferred_element_type=jnp.float32)


def kernel(g, q, m1, m2, rot_o, upd_o, gbuf, qbuf, qstage, qcat, tcat, mbuf, acc, pbuf, dcat, osend, ubuf, dbuf, rbuf, ss, qs, gs, ms, ds, rs, ps, us):
    row, col = lax.axis_index("row"), lax.axis_index("col")
    xh, y, b = row // 8, lax.rem(row // 2, 4), lax.rem(row, 2)
    a, z = col // 8, lax.rem(col, 8)
    x = 2 * xh + a
    o = 1 - b
    cond = {"S": a == b, "N": a != b}
    yy = {d: lax.rem(y + d + 4, 4) for d in (0, 1, -1, 2)}
    zz = {d: lax.rem(z + d + 8, 8) for d in range(-4, 5)}

    def dev(x_, y_, z_, c_):
        return ((x_ // 2) * 8 + y_ * 2 + c_, lax.rem(x_, 2) * 8 + z_)

    px, qx = 2 * xh + 1 - a, lax.rem(x + 2 * a + 3, 4)
    to = {
        "p": dev(px, y, z, b),
        "q": dev(qx, y, z, b),
        "y+": dev(x, yy[1], z, b),
        "y-": dev(x, yy[-1], z, b),
        "z+": dev(x, y, zz[1], b),
        "z-": dev(x, y, zz[-1], b),
        "core": dev(x, y, z, o),
        "swap": dev(2 * xh + b, y, z, o),
        "s+": dev(2 * xh + b, y, zz[1], o),
        "s-": dev(2 * xh + b, y, zz[-1], o),
    }

    def on(tag, f):
        if tag is None:
            f()
        else:
            pl.when(cond[tag])(f)

    sends = []

    def send(tag, src, dst, rsem, where):
        k = len(sends)

        def make():
            return pltpu.make_async_remote_copy(
                src_ref=src(), dst_ref=dst(), send_sem=ss.at[k], recv_sem=rsem(), device_id=to[where], device_id_type=MESH
            )

        make().start()
        sends.append((tag, make))

    def arrived(ref, sem):
        pltpu.make_async_copy(ref, ref, sem).wait()

    def blk(h, d, k):
        return h * 8 + yy[d] * 2 + (o if k else b)

    def near(d, k):
        return lambda: blk(xh, d, k)

    def far(d, k):
        return lambda: blk(1 - xh, d, k)

    def q_part(i, half):
        return qbuf.at[i, pl.ds(*Q_HALF[half]), :]

    def q_send(tag, i, half, *wheres):
        for w in wheres:
            send(tag, lambda: q_part(i(), half), lambda: q_part(i(), half), lambda: qs.at[i(), half], w)

    def q_wait(i, half):
        arrived(q_part(i(), half), qs.at[i(), half])

    def g_part(c, d, half):
        return gbuf.at[c * 8 + zz[d], pl.ds(*G_PART[half]), :]

    def g_send(tag, d, half, *wheres, src=None):
        for w in wheres:
            s = (lambda: g.at[pl.ds(*G_PART[half]), :]) if src else (lambda: g_part(b, d, half))
            send(tag, s, lambda: g_part(b, d, half), lambda: gs.at[b * 8 + zz[d], half], w)

    def g_wait(c, d, half):
        arrived(g_part(c, d, half), gs.at[c * 8 + zz[d], half])

    def pack(put):
        put(0, B, q[:, 0:128])
        put(B, B, q[:, 128:256])
        put(2 * B, 72, jnp.concatenate([q[72 * i : 72 * i + 72, 256:288] for i in range(4)], axis=1))

    def pack_own():
        def put(at, n, v):
            qbuf[row, at : at + n, :] = v

        pack(put)

    def pack_stage():
        def put(at, n, v):
            qstage[at : at + n, :] = v

        pack(put)

    barrier = pltpu.get_barrier_semaphore()

    def greet(*wheres):
        for w in wheres:
            pl.semaphore_signal(barrier, inc=1, device_id=to[w], device_id_type=MESH)

    greet("p", "q", "y+", "y-", "z+", "z-", "core")
    on("N", lambda: greet("swap", "s+", "s-"))
    on("S", pack_own)
    on("N", pack_stage)
    on("S", lambda: pl.semaphore_wait(barrier, 7))
    on("N", lambda: pl.semaphore_wait(barrier, 10))

    own, mate = near(0, 0), near(0, 1)

    def local(half):
        return pltpu.make_async_copy(g.at[pl.ds(*G_PART[half]), :], g_part(b, 0, half), gs.at[b * 8 + z, half])

    def s_first():
        q_send("S", own, 0, "p", "q")
        q_send("S", own, 1, "y+", "y-")
        for j in (0, 1):
            for t in (0, 1):
                g_send("S", 0, FAR_SIDE[t][j], *(("z+", "z-") if t == 0 else ("z-", "z+")), "core", src=True)
        for part in range(4):
            local(part).start()
        pltpu.make_async_copy(m1, mbuf.at[0], ms.at[0]).start()
        pltpu.make_async_copy(m2, mbuf.at[1], ms.at[1]).start()
        q_wait(mate, 0)
        q_send("S", mate, 0, "p", "q")
        q_wait(mate, 1)
        q_send("S", mate, 1, "y-", "y+")
        q_send("S", own, 1, "p", "q")
        q_send("S", own, 0, "y+", "y-")
        q_send("S", mate, 1, "p", "q")
        q_send("S", mate, 0, "y-", "y+")

    def n_first():
        def hand_q(half):
            send("N", lambda: qstage.at[pl.ds(*Q_HALF[half]), :], lambda: q_part(row, half), lambda: qs.at[row, half], "core")

        def hand_g(half):
            send("N", lambda: g.at[pl.ds(*G_PART[half]), :], lambda: g_part(o, 0, half), lambda: gs.at[o * 8 + z, half], "swap")

        hand_q(0)
        hand_q(1)
        for part in (0, 2, 1, 3):
            hand_g(part)

        def first(i, *wheres):
            q_wait(i, 0)
            q_send("N", i, 0, *wheres)

        def ring(half):
            g_wait(b, 0, half)
            g_send("N", 0, half, "z+", "z-", "core")

        ring(0)
        ring(2)
        first(near(0, 0), "q", "y+", "y-")
        first(far(0, 0), "y+", "y-")
        ring(1)
        ring(3)
        first(far(0, 1), "p", "y-", "y+")
        first(near(0, 1), "y-", "y+")

    def s_columns():
        for i, way in ((near(-1, 0), "y+"), (near(1, 1), "y-"), (near(-1, 1), None), (near(1, 0), None)):
            q_wait(i, 1)
            if way:
                q_send("S", i, 1, way)
            q_send("S", i, 1, "p", "q")

    def s_rows():
        q_wait(far(0, 0), 0)
        q_send("S", far(0, 0), 0, "y+", "y-")
        q_wait(far(0, 1), 0)
        q_send("S", far(0, 1), 0, "y-", "y+")

    def z_event(tag, d):
        for fresh in (False, True):
            for j in (0, 1):
                for t, way in enumerate("+-"):
                    part = FAR_SIDE[1 - t if fresh else t][j]
                    hops = 3 if fresh else 4
                    back = d if t else -d
                    if d <= hops:
                        g_wait(b, back, part)
                        g_send(tag, back, part, *((["z" + way] if d < hops else []) + ["core"]))

    def n_columns(d):
        for k in (0, 1):
            q_wait(near(d, k), 1)
            if (d, k) != (0, 1):
                q_send("N", near(d, k), 1, "q")
            q_wait(far(d, k), 1)
            if (d, k) == (0, 1):
                q_send("N", far(d, k), 1, "p")

    def a_ring(tag, h, k):
        for d, way in ((-1, "y+"), (1, "y-")):
            q_wait(h(d, k), 0)
            if way == ("y+", "y-")[k]:
                q_send(tag, h(d, k), 0, way)

    def s_columns_far():
        for k in (0, 1):
            q_wait(near(2, k), 1)
            q_send("S", near(2, k), 1, "p", "q")

    def s_wait(d):
        for k in (0, 1):
            q_wait(far(d, k), 1)

    def moments():
        send("N", lambda: m1, lambda: mbuf.at[0], lambda: ms.at[0], "swap")
        send("N", lambda: m2, lambda: mbuf.at[1], lambda: ms.at[1], "swap")

    def prep(h, *shifts):
        def body(i, carry):
            d = jnp.where(i // 2 == 0, yy[shifts[0]], yy[shifts[-1]])
            k = h * 8 + d * 2 + lax.rem(i, 2)
            tail = qbuf[k, 2 * B : 2 * B + 72, :]
            tail = jnp.concatenate([tail[:, 32 * j : 32 * j + 32] for j in range(4)], axis=0)
            main = jnp.concatenate([qbuf[k, 0:B, :], qbuf[k, B : 2 * B, :]], axis=1)
            hi, lo = split(main)
            tail_hi = tail.astype(jnp.bfloat16).astype(jnp.float32)
            ends = jnp.concatenate([tail_hi, tail_hi, tail - tail_hi], axis=1).astype(jnp.bfloat16)
            qcat[k, :, 0:256] = hi
            qcat[k, :, 256:512] = hi
            qcat[k, :, 512:768] = lo
            qcat[k, :, 768:864] = ends
            hi, lo = split(jnp.concatenate([main, tail], axis=1))
            tcat[k] = jnp.concatenate([hi, hi, lo], axis=0).T
            return carry

        lax.fori_loop(0, 2 * len(shifts), body, 0, unroll=2)

    def group(h, *shifts):
        def body(i, carry):
            d = jnp.where(i // 2 == 0, yy[shifts[0]], yy[shifts[-1]])
            k = h * 8 + d * 2 + lax.rem(i, 2)
            gh, gl = split(gbuf[k])
            acc[...] += dot(tcat[k], jnp.concatenate([gh, gl, gh], axis=0))
            return carry

        lax.fori_loop(0, 2 * len(shifts), body, 0, unroll=2)

    acc[...] = jnp.zeros_like(acc)
    def s_order():
        s_first()
        s_columns()
        z_event("S", 1)
        a_ring("S", near, 0)
        a_ring("S", near, 1)
        s_columns_far()
        z_event("S", 2)
        s_rows()
        prep(xh, 0)
        z_event("S", 3)
        prep(xh, 1, -1)
        a_ring("S", far, 0)
        z_event("S", 4)
        a_ring("S", far, 1)
        for d in (0, 1, -1):
            s_wait(d)
        prep(1 - xh, 0)
        prep(1 - xh, 1, -1)

    def n_order():
        n_first()
        z_event("N", 1)
        n_columns(0)
        a_ring("N", near, 0)
        prep(xh, 0)
        z_event("N", 2)
        n_columns(-1)
        n_columns(1)
        a_ring("N", far, 0)
        a_ring("N", far, 1)
        moments()
        z_event("N", 3)
        a_ring("N", near, 1)
        n_columns(2)
        prep(xh, 1, -1)
        prep(1 - xh, 0)
        prep(1 - xh, 1, -1)
        z_event("N", 4)

    on("S", s_order)
    on("N", n_order)
    for part in range(4):
        on("S", lambda: g_wait(b, 0, part))
    for d in (0, 1, -1, 2, -2, 3, -3, 4):
        for part in range(4):
            g_wait(o, d, part)
    group(xh, 0)
    group(xh, 1, -1)
    group(1 - xh, 0)
    group(1 - xh, 1, -1)
    for k in (0, 1):
        q_wait(near(2, k), 0)
    prep(xh, 2)
    group(xh, 2)
    for k in (0, 1):
        q_wait(far(2, k), 0)
    on("S", lambda: s_wait(2))
    prep(1 - xh, 2)
    group(1 - xh, 2)

    on("S", lambda: rot_o.__setitem__(..., acc[...]))

    @pl.when(cond["N"])
    def _():
        send("N", lambda: acc, lambda: rot_o, lambda: us.at[0], "swap")

    arrived(mbuf.at[0], ms.at[0])
    arrived(mbuf.at[1], ms.at[1])
    rot = acc[...]
    new_first = 0.9 * mbuf[0] + 0.1 * rot
    new_second = 0.999 * mbuf[1] + 0.001 * rot * rot
    direction = new_first / bias_first / (jnp.sqrt(new_second / bias_second) + epsilon)
    hi, lo = split(direction)
    for at, part in enumerate((hi, lo, hi)):
        dcat[256 * at : 256 * at + 256, :] = part[0:256]
        dcat[768 + 32 * at : 800 + 32 * at, :] = part[256:288]
    sums = jnp.broadcast_to(jnp.sum(direction * direction, axis=0, keepdims=True), (8, M))

    def product(c, d, buf):
        j = c * 8 + zz[d]
        buf[d % 8, 0:8, :] = sums
        buf[d % 8, 8:, :] = dot(qcat[j], dcat[...])

    def other(d):
        product(o, d, osend)
        send(None, lambda: osend.at[d % 8], lambda: dbuf.at[d % 8], lambda: ds.at[d % 8], "core")

    def self_(d):
        product(b, d, ubuf)

    def core_sum(*ds_):
        for d in ds_:
            arrived(dbuf.at[d % 8], ds.at[d % 8])

    def came(s, c, k):
        n = U_PART[c][1]
        arrived(rbuf.at[s, c, k, pl.ds(0, n), :], rs.at[s, c, k])
        return rbuf[s, c, k, 0:n, :]

    def link(d, s, c):
        i, (at, n) = d % 8, U_PART[c]
        start = 4 if c in FAR_SIDE[s] else 3
        k = start - abs(d)
        v = ubuf[i, at : at + n, :] + dbuf[i, at : at + n, :]
        if k:
            v = v + came(s, c, k - 1)
        ubuf[i, at : at + n, :] = v

        def go(tag, where):
            send(
                tag,
                lambda: ubuf.at[i, pl.ds(at, n), :],
                lambda: rbuf.at[s, c, k, pl.ds(0, n), :],
                lambda: rs.at[s, c, k],
                where + "+-"[s],
            )

        if abs(d) > 1:
            go(None, "z")
        else:
            on("S", lambda: go("S", "z"))
            on("N", lambda: go("N", "s"))

    def links(d, fresh):
        for j in (0, 1):
            for s in (0, 1):
                link(d if s == 0 else -d, s, FAR_SIDE[1 - s if fresh else s][j])

    other(4)
    self_(4)
    other(3)
    other(-3)
    core_sum(4)
    for j in (0, 1):
        for s in (0, 1):
            link(4, s, FAR_SIDE[s][j])
    self_(3)
    self_(-3)
    core_sum(3, -3)
    links(3, True)
    other(0)
    self_(0)
    other(2)
    other(-2)
    self_(2)
    self_(-2)
    core_sum(0)

    @pl.when(cond["S"])
    def _():
        pbuf[...] = ubuf[0] + dbuf[0]

    @pl.when(cond["N"])
    def _():
        ubuf[0] = ubuf[0] + dbuf[0]
        send("N", lambda: ubuf.at[0], lambda: pbuf, lambda: ps.at[0], "swap")

    links(3, False)
    core_sum(2, -2)
    links(2, True)
    other(1)
    other(-1)
    self_(1)
    self_(-1)
    links(2, False)
    core_sum(1, -1)
    links(1, True)
    links(1, False)
    on("N", lambda: arrived(pbuf, ps.at[0]))

    limit = None
    for c, (at, n) in enumerate(U_PART):
        v = pbuf[at : at + n, :]
        for s in (0, 1):
            v = v + came(s, c, 3 if c in FAR_SIDE[s] else 2)
        if c == 0:
            limit = jnp.maximum(1.0, jnp.sqrt(v[0:1] / D))
            v = v[8:]
        upd_o[72 * c : 72 * c + 72, :] = step_rate * v / limit

    on("N", lambda: arrived(rot_o, us.at[0]))

    for tag in ("S", "N"):

        @pl.when(cond[tag])
        def _():
            for t, make in sends:
                if t == tag:
                    make().wait_send()

    for t, make in sends:
        if t is None:
            make().wait_send()


def solution(mesh):
    def step(gradient, first_moment, second_moment, weights, eigenbasis):
        m1, m2, w = first_moment.T, second_moment.T, weights.T
        f32, bf16 = jnp.float32, jnp.bfloat16
        vmem = pl.BlockSpec(memory_space=pltpu.VMEM)
        hbm = pl.BlockSpec(memory_space=pl.ANY)
        dma = pltpu.SemaphoreType.DMA
        rot, upd = pl.pallas_call(
            kernel,
            out_shape=[jax.ShapeDtypeStruct((B, M), f32)] * 2,
            in_specs=[vmem, vmem, hbm, hbm],
            out_specs=[vmem, vmem],
            scratch_shapes=[
                pltpu.VMEM((NB, B, M), f32),
                pltpu.VMEM((NB, 648, 128), f32),
                pltpu.VMEM((648, 128), f32),
                *[pltpu.VMEM((NB, B, 3 * B), bf16)] * 2,
                pltpu.VMEM((2, B, M), f32),
                pltpu.VMEM((B, M), f32),
                pltpu.VMEM((B + 8, M), f32),
                pltpu.VMEM((3 * B, M), bf16),
                pltpu.VMEM((8, B + 8, M), f32),
                pltpu.VMEM((8, B + 8, M), f32),
                pltpu.VMEM((8, B + 8, M), f32),
                pltpu.VMEM((2, 4, 4, 80, M), f32),
                dma((NSEND,)),
                dma((NB, 2)),
                dma((NB, 4)),
                dma((2,)),
                dma((8,)),
                dma((2, 4, 4)),
                dma((1,)),
                dma((1,)),
            ],
            compiler_params=pltpu.CompilerParams(collective_id=0, has_side_effects=True, vmem_limit_bytes=56 * 2**20),
        )(gradient.T, eigenbasis, m1, m2)
        new_first = 0.9 * m1 + 0.1 * rot
        new_second = 0.999 * m2 + 0.001 * rot * rot
        new_weights = w - upd
        return new_weights.T, new_first.T, new_second.T

    spec = P("row", "col")
    return jax.shard_map(step, mesh=mesh, in_specs=(spec,) * 5, out_specs=(spec,) * 3, check_vma=False)
```

time: 277 us -> 81.5 us (0.29)
  the two profiles are of different devices: /device:TPU:8 before, /device:TPU:1 now
where the time goes in v2:
time: 81.5 us; the launch traced here: 81.4 us
  Pallas kernels  78.7 us (97%)
  other arithmetic  2.01 us (2%)
    pallas_call x1, Pallas kernels, step(): pl.pallas_call(kernel, out_shape=[jax.ShapeDtypeStruct((B, M), f32)] * 2,...  78.7 us
    transpose x1, other arithmetic, step(): return (new_weights.T, new_first.T, new_second.T)  2.01 us

profile of v2, /device:TPU:1, one launch (start us, length us, event | category | flops | bytes accessed | tf_op | source)
XLA Modules:
  0.0 81.4 jit_solution(14219975003357538057)
XLA Ops:
  0.6 0.0 copy-start
  0.6 0.0 copy-start.1
  0.7 0.0 copy-start.2
  0.7 78.7 %shard_map.76 = (f32[288,256]{1,0:T(8,128)}, f32[288,256]{1,0:T(8,128)}) custom-call(f32[288,256]{1,0:T(8,128)} %bitcast.17, f32[288,288]{1,0:T(8,128)} %q.1, f32[288,256]{1,0:T(8,128)} %bitcast.15, f32[288,256]{1,0:T(8,128)} %bitcast.16), custom_call_target="tpu_custom_call" | custom-call | tf_op jit(solution)/shard_map/pallas_call | solution.py:482
  79.3 0.0 copy-done
  79.4 0.0 copy-done.1
  79.4 0.0 copy-done.2
  79.4 2.0 %fusion.1 = (f32[256,288]{0,1:T(8,128)}, f32[256,288]{0,1:T(8,128)}, f32[256,288]{0,1:T(8,128)}) fusion(f32[288,256]{1,0:T(8,128)} %get-tuple-element.6, f32[256,288]{0,1:T(8,128)S(1)} %copy-done.1, f32[256,288]{0,1:T(8,128)S(1)} %copy-done, f32[288,256]{1,0:T(8,128)} %get-tuple-element.5, f32[256,288]{0,1:T(8,128)S(1)} %copy-done.2), kind=kLoop, calls=%fused_computation.2 | loop fusion | flops 589824 | bytes 2359296 | tf_op jit(solution)/shard_map/transpose | solution.py:514
Async XLA Ops:
  0.6 78.7 %copy-start = (f32[256,288]{0,1:T(8,128)S(1)}, f32[256,288]{0,1:T(8,128)}, u32[]{:S(2)}) copy-start(f32[256,288]{0,1:T(8,128)} %param.6) | copy-start | bytes 884740
  0.6 78.7 %copy-start.1 = (f32[256,288]{0,1:T(8,128)S(1)}, f32[256,288]{0,1:T(8,128)}, u32[]{:S(2)}) copy-start(f32[256,288]{0,1:T(8,128)} %param.7) | copy-start | bytes 884740
  0.7 78.7 %copy-start.2 = (f32[256,288]{0,1:T(8,128)S(1)}, f32[256,288]{0,1:T(8,128)}, u32[]{:S(2)}) copy-start(f32[256,288]{0,1:T(8,128)} %param.8) | copy-start | bytes 884740
